TPU v7x, 32 devices: a whole 2x2x4 slice. The times are simulated.
32 devices in a mesh: pop: 8 (over z, x), mp: 4 (over y, core).
Axes of the slice: x: 2, y: 2, z: 4, core: 2. Of those that a mesh axis runs over, the one named last changes fastest.
Arguments:
- tokens: bfloat16 [256, 3584], replicated, may hold values from -60 to 60
- target: bfloat16 [256, 3584], P(None, 'mp'), may hold values from -6 to 6
- w_query: bfloat16 [3584, 3584], P('pop', 'mp'), may hold values from -0.09375 to 0.09375
- w_key: bfloat16 [3584, 512], P(None, 'mp'), may hold values from -0.09375 to 0.09375
- w_value: bfloat16 [3584, 512], P(None, 'mp'), may hold values from -0.09375 to 0.09375
- w_out: bfloat16 [3584, 3584], P('mp', 'pop'), may hold values from -0.09375 to 0.09375
- query_left_factors: bfloat16 [8, 3584, 4], P('pop'), may hold values from -0.09375 to 0.09375
- query_right_factors: bfloat16 [8, 4, 3584], P('pop', None, 'mp'), may hold values from -6 to 6
- o_left: bfloat16 [8, 3584, 4], P('pop', 'mp'), may hold values from -0.09375 to 0.09375
- o_right: bfloat16 [8, 4, 3584], P('pop'), may hold values from -6 to 6
- member_ids: int32 [8], P('pop'), may hold values from 0 to 7, each once
Outputs:
- grad_query: float32 [3584, 3584], P('pop', 'mp')
- grad_out: float32 [3584, 3584], P('mp', 'pop')
- fitness: float32 [8], P('pop')
Inputs may be any that keep to these rules, and one draw needn't show every extreme that they name: `member_ids`: every number from 0 to 7 appears once.
All inputs are finite; a program needn't handle non-finite values.
Results may differ from a plain program's by a relative error of at most 0.005.
Values may be sent and summed in bfloat16 or wider, within the bound.
A program may use at most 64 MiB of HBM per device.

v0:
```python
import math
import jax
import jax.numpy as jnp
from jax import lax
from jax.sharding import PartitionSpec as P

D = 3584
HEADS = 28
KV_HEADS = 4
HEAD_DIM = 128
RANK = 4
noise_scale = 0.5
rope_base = 1000000.0
spread_floor = 0.001


def tables(count, head_size):
    position = jnp.arange(count, dtype=jnp.float32)
    index = jnp.arange(head_size // 2, dtype=jnp.float32)
    freq = jnp.exp(-math.log(rope_base) * 2.0 * index / head_size)
    angle = position[:, None] * freq[None, :]
    return (jnp.cos(angle)[:, None, :], jnp.sin(angle)[:, None, :])


def rotate(field, cosine_table, sine):
    half = field.shape[-1] // 2
    first = field[..., :half]
    second = field[..., half:]
    return jnp.concatenate(
        [first * cosine_table - second * sine, second * cosine_table + first * sine], axis=-1
    )


def per_device(
    tokens,
    target,
    w_query,
    w_key,
    w_value,
    w_out,
    query_left_factors,
    query_right_factors,
    o_left,
    o_right,
    member_ids,
):
    tok = tokens.shape[0]
    local_feats = w_query.shape[1]
    local_kv = w_key.shape[1] // HEAD_DIM
    group = HEADS // KV_HEADS
    local_heads = local_kv * group
    slots = query_left_factors.shape[0]
    scale = HEAD_DIM ** (-0.5)
    cosine_table, sine = tables(tok, HEAD_DIM)
    base = jnp.dot(
        tokens,
        lax.all_gather(w_query, "pop", axis=0, tiled=True),
        preferred_element_type=jnp.float32,
    )
    keys = rotate(
        jnp.dot(tokens, w_key, preferred_element_type=jnp.float32).reshape(tok, local_kv, HEAD_DIM),
        cosine_table,
        sine,
    ).astype(jnp.bfloat16)
    values = (
        jnp.dot(tokens, w_value, preferred_element_type=jnp.float32)
        .astype(jnp.bfloat16)
        .reshape(tok, local_kv, HEAD_DIM)
    )
    signs = (1 - 2 * (member_ids % 2)).astype(jnp.float32)
    factor = noise_scale * signs[:, None, None]
    lowrank_product = jnp.einsum(
        "td,mdr->mtr", tokens, query_left_factors, preferred_element_type=jnp.float32
    ).astype(jnp.bfloat16)
    query = base[None] + factor * jnp.einsum(
        "olj,ojv->olv", lowrank_product, query_right_factors, preferred_element_type=jnp.float32
    )
    query = rotate(
        query.reshape(slots, tok, local_heads, HEAD_DIM), cosine_table[None], sine[None]
    ).astype(jnp.bfloat16)
    query = query.reshape(slots, tok, local_kv, group, HEAD_DIM)
    scores = jnp.einsum("mtkgd,skd->mkgts", query, keys, preferred_element_type=jnp.float32) * scale
    causal = jnp.arange(tok)[:, None] >= jnp.arange(tok)[None, :]
    scores = jnp.where(causal, scores, -1e30)
    probs = jax.nn.softmax(scores, axis=-1).astype(jnp.bfloat16)
    mixed = (
        jnp.einsum("mkgts,skd->mtkgd", probs, values, preferred_element_type=jnp.float32)
        .astype(jnp.bfloat16)
        .reshape(slots, tok, local_feats)
    )
    low_out = jnp.einsum("mtf,mfr->mtr", mixed, o_left, preferred_element_type=jnp.float32)
    right_full = o_right.astype(jnp.float32)
    part = jnp.einsum(
        "mtf,fe->mte",
        mixed,
        lax.all_gather(w_out, "pop", axis=1, tiled=True),
        preferred_element_type=jnp.float32,
    )
    term = part + factor * jnp.einsum(
        "mtr,mre->mte", low_out, right_full, precision=lax.Precision.HIGHEST
    )
    output = lax.psum_scatter(
        term.astype(jnp.bfloat16), "mp", scatter_dimension=2, tiled=True
    ).astype(jnp.float32)
    diff = output - target.astype(jnp.float32)[None]
    errors = lax.psum(jnp.sum(diff * diff, axis=(1, 2)), "mp")
    fitness = -(errors / (tok * D))
    count = slots * lax.axis_size("pop")
    mean = lax.psum(jnp.sum(fitness), "pop") / count
    spread = lax.psum(jnp.sum((fitness - mean) * (fitness - mean)), "pop") / count
    weight = signs * (fitness - mean) / jnp.sqrt(spread + spread_floor)
    every_weight = lax.all_gather(weight, "pop", axis=0, tiled=True)
    right_factors_gathered, left_all = (
        lax.all_gather(query_right_factors, "pop", axis=0, tiled=True),
        lax.all_gather(o_left, "pop", axis=0, tiled=True),
    )
    rows_q = lax.all_to_all(query_left_factors, "pop", split_axis=1, concat_axis=0, tiled=True)
    cols_o = lax.all_to_all(o_right, "pop", split_axis=2, concat_axis=0, tiled=True)
    whole_population = rows_q.shape[0]
    left_q = jnp.transpose(
        rows_q.astype(jnp.float32) * every_weight[:, None, None], (1, 0, 2)
    ).reshape(rows_q.shape[1], whole_population * RANK)
    right_q = right_factors_gathered.astype(jnp.float32).reshape(
        whole_population * RANK, local_feats
    )
    grad_query = jnp.dot(left_q, right_q, precision=lax.Precision.HIGHEST) / noise_scale
    output_left_factor = jnp.transpose(
        left_all.astype(jnp.float32) * every_weight[:, None, None], (1, 0, 2)
    ).reshape(local_feats, whole_population * RANK)
    right_o = cols_o.astype(jnp.float32).reshape(whole_population * RANK, cols_o.shape[2])
    grad_out = jnp.dot(output_left_factor, right_o, precision=lax.Precision.HIGHEST) / noise_scale
    return (grad_query, grad_out, fitness)


def solution(mesh):
    placed = (
        P(),
        P(None, "mp"),
        P("pop", "mp"),
        P(None, "mp"),
        P(None, "mp"),
        P("mp", "pop"),
        P("pop", None, None),
        P("pop", None, "mp"),
        P("pop", "mp", None),
        P("pop", None, None),
        P("pop"),
    )
    return jax.shard_map(
        per_device,
        mesh=mesh,
        in_specs=placed,
        out_specs=(P("pop", "mp"), P("mp", "pop"), P("pop")),
        check_vma=False,
    )
```

profile of v0, /device:TPU:0, one launch (start us, length us, event | category | flops | bytes accessed | tf_op | source)
XLA Modules:
  0.0 465.0 jit_solution(14919115663158646740)
XLA Ops:
  12.2 101.0 %all-gather.3.cloned.1.call-done = bf16[3584,896]{1,0:T(8,128)(2,1)} async-done(((bf16[448,896]{1,0:T(8,128)(2,1)}), bf16[3584,896]{1,0:T(8,128)(2,1)}) %all-gather.3.cloned.1.call-update) | async-done | bytes 6422544 | tf_op jit(solution)/shard_map/all_gather | solution.py:57
  113.2 4.9 %fusion.37 = f32[256,896]{1,0:T(8,128)S(1)} fusion(bf16[256,3584]{1,0:T(8,128)(2,1)S(1)} %copy-done, bf16[3584,896]{1,0:T(8,128)(2,1)} %all-gather.3.cloned.1.call-done), kind=kOutput, calls=%fused_computation.66 | convolution fusion | flops 1644167168 | bytes 9175040 | tf_op jit(solution)/shard_map/dot_general | solution.py:55
  118.1 2.7 fusion.4
  129.5 2.9 convolution_convert_fusion
  132.5 81.4 %all-gather.5.cloned.1.call-done = bf16[896,3584]{0,1:T(8,128)(2,1)} async-done(((bf16[896,448]{0,1:T(8,128)(2,1)}), bf16[896,3584]{0,1:T(8,128)(2,1)}) %all-gather.5.cloned.1.call-update) | async-done | bytes 6422544 | tf_op jit(solution)/shard_map/all_gather | solution.py:96
  213.9 4.9 %fusion.38 = f32[256,3584]{1,0:T(8,128)S(1)} fusion(bf16[256,896]{0,1:T(8,128)(2,1)S(1)} %bitcast.110, bf16[896,3584]{0,1:T(8,128)(2,1)} %all-gather.5.cloned.1.call-done), kind=kOutput, calls=%fused_computation.67 | convolution fusion | flops 1644167168 | bytes 10551296 | tf_op jit(solution)/shard_map/mtf,fe->mte/dot_general | solution.py:93
  218.9 3.7 fusion.2
  222.6 8.8 %copy.54 = bf16[1,256,3584]{1,0,2:T(2,128)(2,1)} copy(bf16[1,256,3584]{2,1,0:T(8,128)(2,1)} %fusion.2) | data formatting | bytes 3670016
  231.4 3.6 copy.62
  235.0 3.2 copy.46
  238.8 20.8 %reduce.4 = bf16[3584,4]{1,0:T(8,128)(2,1)S(1)} reduce(bf16[3584,1,4]{2,1,0:T(2,128)(2,1)} %bitcast.105, bf16[]{:T(256)} %broadcast.87), dimensions={1}, to_apply=%bitcast.83.reduce_sub_computation | reduce | bytes 57346
  259.6 2.2 reshape.258
  261.8 3.6 all-to-all-start.1
  265.4 3.2 copy.37
  268.6 20.7 %reduce.3 = bf16[3584,4]{1,0:T(8,128)(2,1)S(1)} reduce(bf16[3584,1,4]{2,1,0:T(2,128)(2,1)} %bitcast.106, bf16[]{:T(256)} %broadcast.87), dimensions={1}, to_apply=%bitcast.81.reduce_sub_computation | reduce | bytes 57346
  289.3 2.2 reshape.256
  292.2 5.7 %all-to-all-start = ((bf16[8,2,896]{2,1,0:T(2,128)(2,1)}), bf16[8,2,896]{2,1,0:T(2,128)(2,1)S(1)}, u32[]{:S(2)}, u32[]{:S(2)}) async-start(bf16[8,2,896]{2,1,0:T(2,128)(2,1)} %reshape.256), calls=%async_computation | async-start | bytes 57344 | tf_op jit(solution)/shard_map/all_to_all | solution.py:117
  297.8 31.3 %all_gather.19 = bf16[8,896,4]{1,2,0:T(4,128)(2,1)S(1)} all-gather(bf16[1,896,4]{1,2,0:T(4,128)(2,1)S(1)} %copy-done.8), channel_id=1, replica_groups=mesh['pop'=8,'mp'=4] {'pop'}, dimensions={0}, use_global_device_ids=true | all-gather | bytes 64512 | tf_op jit(solution)/shard_map/all_gather | solution.py:115
  329.1 30.7 %all_gather.18 = bf16[8,4,896]{2,1,0:T(4,128)(2,1)S(1)} all-gather(bf16[1,4,896]{2,1,0:T(4,128)(2,1)S(1)} %copy-done.9), channel_id=1, replica_groups=mesh['pop'=8,'mp'=4] {'pop'}, dimensions={0}, use_global_device_ids=true | all-gather | bytes 64512 | tf_op jit(solution)/shard_map/all_gather | solution.py:114
  359.8 3.3 reshape.259
  363.2 3.6 copy.47
  367.0 3.3 reshape.257
  370.3 4.6 bitcast_convert_fusion
  378.0 1.9 fusion.8
  379.8 6.3 %psum.21 = f32[1]{0:T(128)} all-reduce(f32[1]{0:T(128)} %bitcast.27), channel_id=1, replica_groups=mesh['pop'=8,'mp'=4] {'mp'}, use_global_device_ids=true, to_apply=%region_4.5 | all-reduce | flops 1 | bytes 8 | tf_op jit(solution)/shard_map/psum | solution.py:106
  387.2 21.8 %psum.22 = f32[]{:T(128)} all-reduce(f32[]{:T(128)} %bitcast.28), channel_id=1, replica_groups=mesh['pop'=8,'mp'=4] {'pop'}, use_global_device_ids=true, to_apply=%region_5.6 | all-reduce | flops 1 | bytes 8 | tf_op jit(solution)/shard_map/psum | solution.py:109
  412.1 18.3 %psum.23 = f32[]{:T(128)} all-reduce(f32[]{:T(128)} %bitcast.30), channel_id=1, replica_groups=mesh['pop'=8,'mp'=4] {'pop'}, use_global_device_ids=true, to_apply=%region_6.7 | all-reduce | flops 1 | bytes 8 | tf_op jit(solution)/shard_map/psum | solution.py:110
  431.1 1.9 divide_dynamic-update-slice_fusion
  433.0 2.1 copy.44
  435.2 19.1 %all-reduce = f32[8]{0:T(128)S(1)} all-reduce(f32[8]{0:T(128)S(1)} %divide_dynamic-update-slice_fusion), channel_id=1, replica_groups=mesh['pop'=8,'mp'=4] {'pop'}, use_global_device_ids=true, to_apply=%add | all-reduce | flops 8 | bytes 64
  454.4 2.0 convolution_multiply_fusion.1
  456.4 2.1 bitcast_multiply_fusion
  (55 shorter events, 17.5 us)
Async XLA Ops:
  7.2 2.8 copy-start
  7.2 2.8 copy-start.2
  7.2 106.0 %all-gather.3.cloned.1.call-start = ((), (), s32[]{:S(2)}) async-start(), calls=%async_computation.3 | async-start | bytes 7225344 | tf_op jit(solution)/shard_map/all_gather | solution.py:57
  7.9 206.0 %all-gather.5.cloned.1.call-start = ((), (), s32[]{:S(2)}) async-start(), calls=%async_computation.4 | async-start | bytes 7225344 | tf_op jit(solution)/shard_map/all_gather | solution.py:96
  8.7 366.2 %reduce-scatter.4.cloned.1.call-start = ((), (), s32[]{:S(2)}) async-start(), calls=%async_computation.5 | async-start | bytes 2293760
  12.2 105.9 %copy-start.6 = (bf16[1,3584,4]{1,2,0:T(4,128)(2,1)S(1)}, bf16[1,3584,4]{1,2,0:T(4,128)(2,1)}, u32[]{:S(2)}) copy-start(bf16[1,3584,4]{1,2,0:T(4,128)(2,1)} %param.17) | copy-start | bytes 86020
  12.2 105.9 %copy-start.9 = (bf16[1,4,896]{2,1,0:T(4,128)(2,1)S(1)}, bf16[1,4,896]{2,1,0:T(4,128)(2,1)}, u32[]{:S(2)}) copy-start(bf16[1,4,896]{2,1,0:T(4,128)(2,1)} %param.18) | copy-start | bytes 21508
  125.9 1.4 copy-start.3
  125.9 1.4 copy-start.4
  127.9 1.2 copy-start.1
  129.4 2.9 copy-start.8
  132.5 86.4 %copy-start.5 = (bf16[1,4,3584]{2,1,0:T(4,128)(2,1)S(1)}, bf16[1,4,3584]{2,1,0:T(4,128)(2,1)}, u32[]{:S(2)}) copy-start(bf16[1,4,3584]{2,1,0:T(4,128)(2,1)} %param.20) | copy-start | bytes 86020
  238.8 26.6 %copy-start.7 = (bf16[1,3584,4]{1,2,0:T(4,128)(2,1)S(1)}, bf16[1,3584,4]{1,2,0:T(4,128)(2,1)}, u32[]{:S(2)}) copy-start(bf16[1,3584,4]{1,2,0:T(4,128)(2,1)} %param.17) | copy-start | bytes 86020
  261.8 30.4 %all-to-all-start.1 = ((bf16[8,2,896]{2,1,0:T(2,128)(2,1)}), bf16[8,2,896]{2,1,0:T(2,128)(2,1)S(1)}, u32[]{:S(2)}, u32[]{:S(2)}) async-start(bf16[8,2,896]{2,1,0:T(2,128)(2,1)} %reshape.258), calls=%async_computation.1 | async-start | bytes 57344 | tf_op jit(solution)/shard_map/all_to_all | solution.py:118
  268.6 23.0 %copy-start.10 = (u32[32]{0:T(128)S(1)}, u32[32]{0:T(128)}, u32[]{:S(2)}) copy-start(u32[32]{0:T(128)} %constant.59) | copy-start | bytes 388
  292.2 74.8 %all-to-all-start = ((bf16[8,2,896]{2,1,0:T(2,128)(2,1)}), bf16[8,2,896]{2,1,0:T(2,128)(2,1)S(1)}, u32[]{:S(2)}, u32[]{:S(2)}) async-start(bf16[8,2,896]{2,1,0:T(2,128)(2,1)} %reshape.256), calls=%async_computation | async-start | bytes 57344 | tf_op jit(solution)/shard_map/all_to_all | solution.py:117
Sparse Core Ops, SparseCore 0:
  10.2 103.0 all-gather.2
  115.4 98.4 all-gather.4
  235.2 27.7 reduce-scatter.3
where the time goes:
time: 466 us; the launch traced here: 465 us
  waiting for transfers between devices  184 us (39%)
  blocking collectives  127 us (27%)
  other arithmetic  53.7 us (12%)
  local copies, waits for them, and re-layouts  46.4 us (10%)
  matrix products  24.7 us (5%)
  between operations  19.6 us (4%)
  starting transfers between devices  9.34 us (2%)
    all_gather x1, waiting for transfers between devices, per_device(): lax.all_gather(w_query, 'pop', axis=0, tiled=True)  101 us
    all_gather x1, waiting for transfers between devices, per_device(): lax.all_gather(w_out, 'pop', axis=1, tiled=True)  81.4 us
    unnamed x3, other arithmetic  43.4 us
    unnamed x37, local copies, waits for them, and re-layouts  38 us
    all_gather x1, blocking collectives, per_device(): lax.all_gather(o_left, 'pop', axis=0, tiled=True)  31.3 us
    all_gather x1, blocking collectives, per_device(): lax.all_gather(query_right_factors, 'pop', axis=0, tiled=True)  30.7 us
    psum x1, blocking collectives, per_device(): mean = lax.psum(jnp.sum(fitness), 'pop') / count  21.8 us
    unnamed x1, blocking collectives  19.1 us
  transfers between devices with their start and end apart: 5, of which 2 were waited for; matrix products, arithmetic and copies ran while one was open for 19% of the time, Pallas kernels for 0%

commit v1 on v0

--- a/solution.py
+++ b/solution.py
@@ -93,7 +93,7 @@
     part = jnp.einsum(
         "mtf,fe->mte",
         mixed,
-        lax.all_gather(w_out, "pop", axis=1, tiled=True),
+        jnp.concatenate(lax.all_gather(w_out, "pop"), axis=1),
         preferred_element_type=jnp.float32,
     )
     term = part + factor * jnp.einsum(

time: 466 us -> 466 us (level)
  waiting for transfers between devices: 184 us -> 190 us
  other arithmetic: 53.7 us -> 48.9 us
    all_gather x1, waiting for transfers between devices: 81.4 us -> 87.5 us  [per_device(): lax.all_gather(w_out, 'pop')]
    unnamed x37 -> x46, local copies, waits for them, and re-layouts: 38 us -> 37.6 us
  transfers between devices with their start and end apart: 5 -> 5, of which waited for: 2 -> 2; matrix products, arithmetic and copies ran while one was open for 19% -> 16% of each run, Pallas kernels for 0% -> 0%
where the time goes in v1:
time: 466 us; the launch traced here: 465 us
  waiting for transfers between devices  190 us (41%)
  blocking collectives  127 us (27%)
  other arithmetic  48.9 us (10%)
  local copies, waits for them, and re-layouts  46.4 us (10%)
  matrix products  23.2 us (5%)
  between operations  19.7 us (4%)
  starting transfers between devices  9.46 us (2%)
    all_gather x1, waiting for transfers between devices, per_device(): lax.all_gather(w_query, 'pop', axis=0, tiled=True)  101 us
    all_gather x1, waiting for transfers between devices, per_device(): lax.all_gather(w_out, 'pop')  87.5 us
    unnamed x3, other arithmetic  41.4 us
    unnamed x46, local copies, waits for them, and re-layouts  37.6 us
    all_gather x1, blocking collectives, per_device(): lax.all_gather(o_left, 'pop', axis=0, tiled=True)  31.3 us
    all_gather x1, blocking collectives, per_device(): lax.all_gather(query_right_factors, 'pop', axis=0, tiled=True)  30.7 us
    psum x1, blocking collectives, per_device(): mean = lax.psum(jnp.sum(fitness), 'pop') / count  21.8 us
    unnamed x1, blocking collectives  19.1 us
  transfers between devices with their start and end apart: 5, of which 2 were waited for; matrix products, arithmetic and copies ran while one was open for 16% of the time, Pallas kernels for 0%

profile of v1, /device:TPU:0, one launch (start us, length us, event | category | flops | bytes accessed | tf_op | source)
XLA Modules:
  0.0 464.9 jit_solution(4772980862311053942)
XLA Ops:
  12.2 101.0 %all-gather.4.cloned.1.call-done = bf16[3584,896]{1,0:T(8,128)(2,1)} async-done(((bf16[448,896]{1,0:T(8,128)(2,1)}), bf16[3584,896]{1,0:T(8,128)(2,1)}) %all-gather.4.cloned.1.call-update) | async-done | bytes 6422544 | tf_op jit(solution)/shard_map/all_gather | solution.py:57
  113.2 4.9 %fusion.37 = f32[256,896]{1,0:T(8,128)S(1)} fusion(bf16[256,3584]{1,0:T(8,128)(2,1)S(1)} %copy-done, bf16[3584,896]{1,0:T(8,128)(2,1)} %all-gather.4.cloned.1.call-done), kind=kOutput, calls=%fused_computation.66 | convolution fusion | flops 1644167168 | bytes 9175040 | tf_op jit(solution)/shard_map/dot_general | solution.py:55
  118.1 2.7 fusion.4
  125.9 87.5 %all-gather.6.cloned.1.call-done = bf16[7168,448]{0,1:T(8,128)(2,1)} async-done(((bf16[896,448]{0,1:T(8,128)(2,1)}), bf16[7168,448]{0,1:T(8,128)(2,1)}) %all-gather.6.cloned.1.call-update) | async-done | bytes 6422544 | tf_op jit(solution)/shard_map/all_gather | solution.py:96
  213.3 4.3 copy.70
  217.6 3.8 copy.54
  224.6 2.6 convolution_convert_fusion
  227.2 4.9 %fusion.38 = f32[256,3584]{1,0:T(8,128)S(1)} fusion(bf16[256,896]{0,1:T(8,128)(2,1)S(1)} %bitcast.119, bf16[896,3584]{0,1:T(8,128)(2,1)} %bitcast.109), kind=kOutput, calls=%fused_computation.67 | convolution fusion | flops 1644167168 | bytes 10551296 | tf_op jit(solution)/shard_map/mtf,fe->mte/dot_general | solution.py:93
  232.3 2.5 fusion.2
  234.8 6.5 %copy.65 = bf16[1,256,3584]{1,0,2:T(2,128)(2,1)} copy(bf16[1,256,3584]{2,1,0:T(8,128)(2,1)S(1)} %fusion.2) | data formatting | bytes 3670016
  241.3 3.6 copy.74
  244.9 2.5 copy.57
  248.0 19.7 %reduce.4 = bf16[3584,4]{1,0:T(8,128)(2,1)S(1)} reduce(bf16[3584,1,4]{2,1,0:T(2,128)(2,1)S(1)} %bitcast.114, bf16[]{:T(256)} %broadcast.87), dimensions={1}, to_apply=%bitcast.90.reduce_sub_computation | reduce | bytes 57346
  267.7 2.2 reshape.267
  269.9 3.6 all-to-all-start.1
  273.5 2.5 copy.47
  276.1 19.7 %reduce.3 = bf16[3584,4]{1,0:T(8,128)(2,1)S(1)} reduce(bf16[3584,1,4]{2,1,0:T(2,128)(2,1)S(1)} %bitcast.115, bf16[]{:T(256)} %broadcast.87), dimensions={1}, to_apply=%bitcast.88.reduce_sub_computation | reduce | bytes 57346
  295.8 2.2 reshape.265
  298.6 5.8 %all-to-all-start = ((bf16[8,2,896]{2,1,0:T(2,128)(2,1)}), bf16[8,2,896]{2,1,0:T(2,128)(2,1)S(1)}, u32[]{:S(2)}, u32[]{:S(2)}) async-start(bf16[8,2,896]{2,1,0:T(2,128)(2,1)} %reshape.265), calls=%async_computation | async-start | bytes 57344 | tf_op jit(solution)/shard_map/all_to_all | solution.py:117
  304.4 31.3 %all_gather.23 = bf16[8,896,4]{1,2,0:T(4,128)(2,1)S(1)} all-gather(bf16[1,896,4]{1,2,0:T(4,128)(2,1)S(1)} %copy-done.11), channel_id=1, replica_groups=mesh['pop'=8,'mp'=4] {'pop'}, dimensions={0}, use_global_device_ids=true | all-gather | bytes 64512 | tf_op jit(solution)/shard_map/all_gather | solution.py:115
  335.6 30.7 %all_gather.22 = bf16[8,4,896]{2,1,0:T(4,128)(2,1)S(1)} all-gather(bf16[1,4,896]{2,1,0:T(4,128)(2,1)S(1)} %copy-done.12), channel_id=1, replica_groups=mesh['pop'=8,'mp'=4] {'pop'}, dimensions={0}, use_global_device_ids=true | all-gather | bytes 64512 | tf_op jit(solution)/shard_map/all_gather | solution.py:114
  366.4 2.3 reshape.268
  370.7 2.4 reshape.266
  373.1 3.0 bitcast_convert_fusion
  379.3 1.9 fusion.8
  381.2 6.3 %psum.21 = f32[1]{0:T(128)} all-reduce(f32[1]{0:T(128)} %bitcast.29), channel_id=1, replica_groups=mesh['pop'=8,'mp'=4] {'mp'}, use_global_device_ids=true, to_apply=%region_4.5 | all-reduce | flops 1 | bytes 8 | tf_op jit(solution)/shard_map/psum | solution.py:106
  388.6 21.8 %psum.22 = f32[]{:T(128)} all-reduce(f32[]{:T(128)} %bitcast.30), channel_id=1, replica_groups=mesh['pop'=8,'mp'=4] {'pop'}, use_global_device_ids=true, to_apply=%region_5.6 | all-reduce | flops 1 | bytes 8 | tf_op jit(solution)/shard_map/psum | solution.py:109
  413.5 18.3 %psum.23 = f32[]{:T(128)} all-reduce(f32[]{:T(128)} %bitcast.32), channel_id=1, replica_groups=mesh['pop'=8,'mp'=4] {'pop'}, use_global_device_ids=true, to_apply=%region_6.7 | all-reduce | flops 1 | bytes 8 | tf_op jit(solution)/shard_map/psum | solution.py:110
  432.5 2.0 divide_dynamic-update-slice_fusion
  435.1 19.1 %all-reduce = f32[8]{0:T(128)S(1)} all-reduce(f32[8]{0:T(128)S(1)} %divide_dynamic-update-slice_fusion), channel_id=1, replica_groups=mesh['pop'=8,'mp'=4] {'pop'}, use_global_device_ids=true, to_apply=%add | all-reduce | flops 8 | bytes 64
  454.4 2.0 convolution_multiply_fusion.1
  456.3 2.1 bitcast_multiply_fusion
  (65 shorter events, 19.8 us)
Async XLA Ops:
  7.2 2.8 copy-start
  7.2 2.8 copy-start.5
  7.2 106.0 %all-gather.4.cloned.1.call-start = ((), (), s32[]{:S(2)}) async-start(), calls=%async_computation.3 | async-start | bytes 7225344 | tf_op jit(solution)/shard_map/all_gather | solution.py:57
  7.9 205.4 %all-gather.6.cloned.1.call-start = ((), (), s32[]{:S(2)}) async-start(), calls=%async_computation.4 | async-start | bytes 7225344 | tf_op jit(solution)/shard_map/all_gather | solution.py:96
  8.7 367.4 %reduce-scatter.4.cloned.1.call-start = ((), (), s32[]{:S(2)}) async-start(), calls=%async_computation.5 | async-start | bytes 2293760
  12.2 105.9 %copy-start.9 = (bf16[1,3584,4]{1,2,0:T(4,128)(2,1)S(1)}, bf16[1,3584,4]{1,2,0:T(4,128)(2,1)}, u32[]{:S(2)}) copy-start(bf16[1,3584,4]{1,2,0:T(4,128)(2,1)} %param.17) | copy-start | bytes 86020
  12.2 105.9 %copy-start.12 = (bf16[1,4,896]{2,1,0:T(4,128)(2,1)S(1)}, bf16[1,4,896]{2,1,0:T(4,128)(2,1)}, u32[]{:S(2)}) copy-start(bf16[1,4,896]{2,1,0:T(4,128)(2,1)} %param.18) | copy-start | bytes 21508
  217.6 3.8 copy-start.4
  221.4 0.8 copy-start.6
  221.4 0.8 copy-start.7
  222.8 1.3 copy-start.3
  222.8 1.8 copy-start.13
  227.2 5.0 %copy-start.11 = (bf16[1,896,4]{1,2,0:T(4,128)(2,1)S(1)}, bf16[1,896,4]{1,2,0:T(4,128)(2,1)}, u32[]{:S(2)}) copy-start(bf16[1,896,4]{1,2,0:T(4,128)(2,1)} %param.19) | copy-start | bytes 21508
  227.2 5.1 %copy-start.8 = (bf16[1,4,3584]{2,1,0:T(4,128)(2,1)S(1)}, bf16[1,4,3584]{2,1,0:T(4,128)(2,1)}, u32[]{:S(2)}) copy-start(bf16[1,4,3584]{2,1,0:T(4,128)(2,1)} %param.20) | copy-start | bytes 86020
  248.0 25.5 %copy-start.10 = (bf16[1,3584,4]{1,2,0:T(4,128)(2,1)S(1)}, bf16[1,3584,4]{1,2,0:T(4,128)(2,1)}, u32[]{:S(2)}) copy-start(bf16[1,3584,4]{1,2,0:T(4,128)(2,1)} %param.17) | copy-start | bytes 86020
  269.9 28.7 %all-to-all-start.1 = ((bf16[8,2,896]{2,1,0:T(2,128)(2,1)}), bf16[8,2,896]{2,1,0:T(2,128)(2,1)S(1)}, u32[]{:S(2)}, u32[]{:S(2)}) async-start(bf16[8,2,896]{2,1,0:T(2,128)(2,1)} %reshape.267), calls=%async_computation.1 | async-start | bytes 57344 | tf_op jit(solution)/shard_map/all_to_all | solution.py:118
  276.0 21.9 %copy-start.14 = (u32[32]{0:T(128)S(1)}, u32[32]{0:T(128)}, u32[]{:S(2)}) copy-start(u32[32]{0:T(128)} %constant.59) | copy-start | bytes 388
  298.6 72.1 %all-to-all-start = ((bf16[8,2,896]{2,1,0:T(2,128)(2,1)}), bf16[8,2,896]{2,1,0:T(2,128)(2,1)S(1)}, u32[]{:S(2)}, u32[]{:S(2)}) async-start(bf16[8,2,896]{2,1,0:T(2,128)(2,1)} %reshape.265), calls=%async_computation | async-start | bytes 57344 | tf_op jit(solution)/shard_map/all_to_all | solution.py:117
  376.1 58.3 %copy-start.2 = (f32[1,3584,4]{2,0,1:T(1,128)S(1)}, f32[1,3584,4]{2,0,1:T(1,128)}, u32[]{:S(2)}) copy-start(f32[1,3584,4]{2,0,1:T(1,128)} %bitcast_convert_fusion) | copy-start | bytes 172036
  454.3 4.1 copy-start.1
Sparse Core Ops, SparseCore 0:
  10.2 103.0 all-gather.3
  115.4 97.9 all-gather.5
  245.1 28.3 reduce-scatter.3
